TPU v7x, 32 devices: a whole 2x2x4 slice. The times are simulated.
32 devices in a mesh: px: 4 (over y, x), py: 8 (over z, core).
Axes of the slice: x: 2, y: 2, z: 4, core: 2. Of those that a mesh axis runs over, the one named last changes fastest.
Arguments:
- velocity: float32 [3, 8, 256, 1024], P(None, None, 'py', 'px'), may hold values from -6 to 6
- thickness: float32 [8, 256, 1024], P(None, 'py', 'px'), may hold values from 1 to 4
- velocity_tendency: float32 [3, 8, 256, 1024], P(None, None, 'py', 'px'), may hold values from -6 to 6
- thickness_tendency: float32 [8, 256, 1024], P(None, 'py', 'px'), may hold values from -0.5 to 0.5
- cell_distance: float32 [3, 256, 1024], P(None, 'py', 'px'), may hold values from 0.5 to 2
- edge_length: float32 [3, 256, 1024], P(None, 'py', 'px'), may hold values from 0.5 to 2
- cell_area: float32 [256, 1024], P('py', 'px'), may hold values from 1 to 4
- kite_area: float32 [2, 3, 256, 1024], P(None, None, 'py', 'px'), may hold values from 0.2 to 0.8
- coriolis: float32 [2, 256, 1024], P(None, 'py', 'px'), may hold values from -1 to 1
Outputs:
- vertex_potential: float32 [2, 8, 256, 1024], P(None, None, 'py', 'px')
- kinetic_energy: float32 [8, 256, 1024], P(None, 'py', 'px')
- cell_potential: float32 [8, 256, 1024], P(None, 'py', 'px')
- edge_potential: float32 [3, 8, 256, 1024], P(None, None, 'py', 'px')
All inputs are finite; a program needn't handle non-finite values.
Results may differ from a plain program's by a relative error of at most 0.00002.
Values sent between devices are 32-bit elements; how exact they have to be, the bound alone decides.
A program may use at most 64 MiB of HBM per device.

v0:
```python
import jax
import jax.numpy as jnp
from jax import lax
from jax.sharding import PartitionSpec as P

SECTIONS = 4


SECTION_STEP = (0.0, 0.5, 0.5, 1.0)
SECTION_WEIGHT = (1.0 / 6.0, 1.0 / 3.0, 1.0 / 3.0, 1.0 / 6.0)
UPWIND_FACTOR = 0.5


def with_halo(cells, sides, width):
    for axis, dim in sides:
        count = lax.axis_size(axis)
        head = lax.slice_in_dim(cells, 0, width, axis=dim)
        tail = lax.slice_in_dim(cells, cells.shape[dim] - width, cells.shape[dim], axis=dim)
        cells = jnp.concatenate(
            [
                lax.ppermute(tail, axis, [(i, (i + 1) % count) for i in range(count)]),
                cells,
                lax.ppermute(head, axis, [((i + 1) % count, i) for i in range(count)]),
            ],
            axis=dim,
        )
    return cells


def offset(padded, margin, first_off, second_off):
    row_count = padded.shape[-2] - 2 * margin
    col_count = padded.shape[-1] - 2 * margin
    return padded[
        ...,
        margin + first_off : margin + first_off + row_count,
        margin + second_off : margin + second_off + col_count,
    ]


def window(padded, row_start, col_start, row_count, col_count):
    return padded[..., row_start : row_start + row_count, col_start : col_start + col_count]


def cell_mean_extended(vertex_pad, row_count, col_count):
    first = vertex_pad[0]
    second = vertex_pad[1]
    cols = col_count + 1
    return (
        window(first, 1, 1, row_count, cols)
        + window(second, 1, 1, row_count, cols)
        + window(first, 0, 1, row_count, cols)
        + window(first, 1, 0, row_count, cols)
        + window(second, 1, 0, row_count, cols)
        + window(second, 2, 0, row_count, cols)
    ) / 6.0


def local(
    velocity,
    thickness,
    velocity_tendency,
    thickness_tendency,
    cell_distance,
    edge_length,
    cell_area,
    kite_area,
    coriolis,
):
    levels = thickness.shape[0]
    row_count = thickness.shape[1]
    col_count = thickness.shape[2]
    rim_width = 1
    geometry = jnp.concatenate([cell_distance, 0.25 * cell_distance * edge_length], axis=0)
    geometry_pad = with_halo(geometry, (("px", 2), ("py", 1)), rim_width)
    triangle_area = jnp.sum(kite_area, axis=1)
    padded_shape = (row_count + 2 * rim_width, col_count + 2 * rim_width)
    joined = jnp.concatenate(
        [
            velocity.reshape(3 * levels, row_count, col_count),
            thickness,
            velocity_tendency.reshape(3 * levels, row_count, col_count),
            thickness_tendency,
        ],
        axis=0,
    )
    joined_pad = with_halo(joined, (("px", 2), ("py", 1)), rim_width)
    base_count = 4 * levels
    vertex_total = jnp.zeros((2,) + thickness.shape, jnp.float32)
    energy_total = jnp.zeros(thickness.shape, jnp.float32)
    cell_total = jnp.zeros(thickness.shape, jnp.float32)
    edge_total = jnp.zeros(velocity.shape, jnp.float32)
    for section_index in range(SECTIONS):
        step_size = SECTION_STEP[section_index]
        weight_now = SECTION_WEIGHT[section_index]
        velocity_pad = joined_pad[0 : 3 * levels].reshape(
            (3, levels) + padded_shape
        ) + step_size * joined_pad[base_count : base_count + 3 * levels].reshape(
            (3, levels) + padded_shape
        )
        thickness_pad = (
            joined_pad[3 * levels : base_count] + step_size * joined_pad[base_count + 3 * levels :]
        )
        inner_velocity = offset(velocity_pad, rim_width, 0, 0)
        edge_flux = velocity_pad * geometry_pad[0:3][:, None]
        circulation_first = (
            offset(edge_flux[0], 1, 0, 0)
            + offset(edge_flux[2], 1, 1, 0)
            - offset(edge_flux[1], 1, 0, 0)
        )
        circulation_second = (
            offset(edge_flux[1], 1, 0, 0)
            - offset(edge_flux[2], 1, 0, 0)
            - offset(edge_flux[0], 1, -1, 1)
        )
        height_first = (
            kite_area[0, 0] * offset(thickness_pad, 1, 0, 0)
            + kite_area[0, 1] * offset(thickness_pad, 1, 1, 0)
            + kite_area[0, 2] * offset(thickness_pad, 1, 0, 1)
        ) / triangle_area[0]
        height_second = (
            kite_area[1, 0] * offset(thickness_pad, 1, 0, 0)
            + kite_area[1, 1] * offset(thickness_pad, 1, 0, 1)
            + kite_area[1, 2] * offset(thickness_pad, 1, -1, 1)
        ) / triangle_area[1]
        potential_first = (coriolis[0] + circulation_first / triangle_area[0]) / height_first
        potential_second = (coriolis[1] + circulation_second / triangle_area[1]) / height_second
        energy_pad = geometry_pad[3:6][:, None] * velocity_pad * velocity_pad
        kinetic = (
            offset(energy_pad[0], rim_width, 0, 0)
            + offset(energy_pad[1], rim_width, 0, 0)
            + offset(energy_pad[2], rim_width, 0, 0)
            + offset(energy_pad[0], rim_width, -1, 0)
            + offset(energy_pad[1], rim_width, 0, -1)
            + offset(energy_pad[2], rim_width, 1, -1)
        ) / cell_area
        wide_pair = jnp.stack([potential_first, potential_second])
        vertex_pair = offset(wide_pair, rim_width - 1, 0, 0)
        flat_pair = vertex_pair.reshape(2 * levels, row_count, col_count)
        vertex_pad = with_halo(flat_pair, (("px", 2), ("py", 1)), 1).reshape(
            (2, levels, row_count + 2, col_count + 2)
        )
        cell_extended = cell_mean_extended(vertex_pad, row_count, col_count)
        cell_value = cell_extended[..., 0:col_count]
        cell_rows = with_halo(cell_extended, (("py", 1),), 1)
        vertex_margin = 1
        cell_below = window(cell_rows, 2, 0, row_count, col_count)
        cell_right = window(cell_rows, 1, 1, row_count, col_count)
        cell_diagonal = window(cell_rows, 0, 1, row_count, col_count)
        mean_zero = 0.5 * (
            offset(vertex_pad[0], vertex_margin, 0, 0) + offset(vertex_pad[1], vertex_margin, 1, -1)
        )
        mean_one = 0.5 * (
            offset(vertex_pad[0], vertex_margin, 0, 0) + offset(vertex_pad[1], vertex_margin, 0, 0)
        )
        mean_two = 0.5 * (
            offset(vertex_pad[1], vertex_margin, 0, 0) + offset(vertex_pad[0], vertex_margin, -1, 0)
        )
        grad_zero = (cell_below - cell_value) / cell_distance[0]
        grad_one = (cell_right - cell_value) / cell_distance[1]
        grad_two = (cell_diagonal - cell_value) / cell_distance[2]
        section_edge = jnp.stack(
            [
                mean_zero - UPWIND_FACTOR * inner_velocity[0] * grad_zero,
                mean_one - UPWIND_FACTOR * inner_velocity[1] * grad_one,
                mean_two - UPWIND_FACTOR * inner_velocity[2] * grad_two,
            ]
        )
        vertex_total = vertex_total + weight_now * vertex_pair
        energy_total = energy_total + weight_now * kinetic
        cell_total = cell_total + weight_now * cell_value
        edge_total = edge_total + weight_now * section_edge
    return (vertex_total, energy_total, cell_total, edge_total)


def solution(mesh):
    placed = (
        P(None, None, "py", "px"),
        P(None, "py", "px"),
        P(None, None, "py", "px"),
        P(None, "py", "px"),
        P(None, "py", "px"),
        P(None, "py", "px"),
        P("py", "px"),
        P(None, None, "py", "px"),
        P(None, "py", "px"),
    )
    return jax.shard_map(
        local,
        mesh=mesh,
        in_specs=placed,
        out_specs=(
            P(None, None, "py", "px"),
            P(None, "py", "px"),
            P(None, "py", "px"),
            P(None, None, "py", "px"),
        ),
        check_vma=False,
    )
```

profile of v0, /device:TPU:0, one launch (start us, length us, event | category | flops | bytes accessed | tf_op | source)
XLA Modules:
  0.0 96.2 jit_solution(16507078211564368692)
XLA Ops:
  0.6 1.0 multiply_multiply_fusion.3
  1.6 0.9 fusion.133
  2.5 3.0 %collective-permute-start.4 = (f32[6,32,1]{2,1,0:T(8,128)S(1)}, f32[6,32,1]{2,1,0:T(8,128)S(1)}, u32[]{:S(2)}, u32[]{:S(2)}) collective-permute-start(f32[6,32,1]{2,1,0:T(8,128)S(1)} %get-tuple-element.84), channel_id=1, source_target_pairs={{0,8},{8,16},{16,24},{24,0},{1,9},{9,17},{17,25},{25,1},{2,10},{10... | collective-permute-start | bytes 2312 | tf_op jit(solution)/shard_map/ppermute | solution.py:21
  5.5 1.0 %collective-permute-start.5 = (f32[6,32,1]{2,1,0:T(8,128)S(1)}, f32[6,32,1]{2,1,0:T(8,128)S(1)}, u32[]{:S(2)}, u32[]{:S(2)}) collective-permute-start(f32[6,32,1]{2,1,0:T(8,128)S(1)} %get-tuple-element.85), channel_id=1, source_target_pairs={{8,0},{16,8},{24,16},{0,24},{9,1},{17,9},{25,17},{1,25},{10,2},{18... | collective-permute-start | bytes 2312 | tf_op jit(solution)/shard_map/ppermute | solution.py:23
  6.5 1.7 %pad_maximum_fusion.1 = f32[64,32,256]{2,1,0:T(8,128)S(1)} fusion(f32[8,32,256]{2,1,0:T(8,128)} %param.12, f32[24,32,256]{2,1,0:T(8,128)} %bitcast.144, f32[8,32,256]{2,1,0:T(8,128)} %param.10, f32[24,32,256]{2,1,0:T(8,128)} %bitcast.147), kind=kLoop, calls=%fused_computation.4 | loop fusion | flops 1572864 | bytes 4194304 | tf_op jit(solution)/shard_map/concatenate | solution.py:77
  8.6 0.6 copy.38
  9.3 2.0 %collective-permute-start.1 = (f32[64,32,1]{0,1,2:T(8,128)S(1)}, f32[64,32,1]{0,1,2:T(8,128)}, u32[]{:S(2)}, u32[]{:S(2)}) collective-permute-start(f32[64,32,1]{0,1,2:T(8,128)S(1)} %copy.38), channel_id=1, source_target_pairs={{8,0},{16,8},{24,16},{0,24},{9,1},{17,9},{25,17},{1,25},{10,2},{18... | collective-permute-start | bytes 24584 | tf_op jit(solution)/shard_map/ppermute | solution.py:23
  11.2 0.6 copy.37
  11.9 0.6 slice_bitcast_fusion.29
  12.6 0.7 slice_bitcast_fusion.19
  13.5 3.5 %collective-permute-start.7 = (f32[6,1,258]{2,1,0:T(1,128)S(1)}, f32[6,1,258]{2,1,0:T(1,128)S(1)}, u32[]{:S(2)}, u32[]{:S(2)}) collective-permute-start(f32[6,1,258]{2,1,0:T(1,128)S(1)} %get-tuple-element.75), channel_id=1, source_target_pairs={{1,0},{2,1},{3,2},{4,3},{5,4},{6,5},{7,6},{0,7},{9,8},{10,9},{11,1... | collective-permute-start | bytes 18584 | tf_op jit(solution)/shard_map/ppermute | solution.py:23
  17.0 0.6 slice_bitcast_fusion.22
  17.6 0.7 collective-permute-done.6
  18.4 0.9 pad_maximum_fusion.11
  19.3 1.0 %copy.39 = f32[64,32,1]{2,1,0:T(8,128)S(1)} copy(f32[64,32,1]{0,1,2:T(8,128)S(1)} %collective-permute-done) | data formatting | bytes 16384 | tf_op jit(solution)/shard_map/ppermute | solution.py:21
  20.3 1.7 %copy.40 = f32[64,32,1]{2,1,0:T(8,128)S(1)} copy(f32[64,32,1]{0,1,2:T(8,128)} %collective-permute-done.1) | data formatting | bytes 16384 | tf_op jit(solution)/shard_map/ppermute | solution.py:23
  22.0 1.7 %pad_maximum_fusion.42 = (f32[64,1,258]{2,1,0:T(1,128)S(1)}, f32[64,1,258]{2,1,0:T(1,128)S(1)}) fusion(f32[64,32,1]{2,1,0:T(8,128)S(1)} %copy.40, f32[64,32,1]{2,1,0:T(8,128)S(1)} %copy.39, f32[8,32,256]{2,1,0:T(8,128)S(1)} %copy-done.3, f32[24,32,256]{2,1,0:T(8,128)S(1)} %bitcast.145, f32[8,32,256]{2,1,0:T(8,128)S(1)} %copy-done.4, f32[24,32,256]{2,1,0:T(8,128)} %bitcast.148), kind=kLoop, calls=%fused_computation.268 | loop fusion | flops 165120 | bytes 2245632 | tf_op jit(solution)/shard_map/slice | solution.py:18
  24.1 3.5 %collective-permute-start.3 = (f32[64,1,258]{2,1,0:T(1,128)S(1)}, f32[64,1,258]{2,1,0:T(1,128)S(1)}, u32[]{:S(2)}, u32[]{:S(2)}) collective-permute-start(f32[64,1,258]{2,1,0:T(1,128)S(1)} %get-tuple-element.15), channel_id=1, source_target_pairs={{1,0},{2,1},{3,2},{4,3},{5,4},{6,5},{7,6},{0,7},{9,8},{10,9},{11,1... | collective-permute-start | bytes 198152 | tf_op jit(solution)/shard_map/ppermute | solution.py:23
  27.6 2.2 %collective-permute-done.2 = f32[64,1,258]{2,1,0:T(1,128)S(1)} collective-permute-done((f32[64,1,258]{2,1,0:T(1,128)S(1)}, f32[64,1,258]{2,1,0:T(1,128)S(1)}, u32[]{:S(2)}, u32[]{:S(2)}) %collective-permute-start.2) | collective-permute-done | bytes 66080 | tf_op jit(solution)/shard_map/ppermute | solution.py:21
  29.8 6.1 %pad_maximum_fusion = f32[64,34,258]{2,1,0:T(8,128)S(1)} fusion(f32[64,1,258]{2,1,0:T(1,128)S(1)} %collective-permute-done.3, f32[64,32,1]{2,1,0:T(8,128)S(1)} %copy.40, f32[8,32,256]{2,1,0:T(8,128)S(1)} %copy-done.3, f32[24,32,256]{2,1,0:T(8,128)S(1)} %bitcast.146, f32[8,32,256]{2,1,0:T(8,128)S(1)} %copy-done.4, f32[24,32,256]{2,1,0:T(8,128)S(1)} %bitcast.149, ...), kind=kLoop, calls=%fused_computation | loop fusion | flops 3929856 | bytes 4491264 | tf_op jit(solution)/shard_map/concatenate | solution.py:19
  36.2 0.9 multiply_multiply_fusion.2
  38.4 0.5 fusion.98
  38.9 0.5 fusion.104
  39.4 1.0 %fusion.128 = (f32[8,32,256]{2,1,0:T(8,128)S(1)}, f32[8,32,256]{2,1,0:T(8,128)S(1)}) fusion(f32[8,34,258]{2,1,0:T(8,128)S(1)} %get-tuple-element.16, f32[8,34,258]{2,1,0:T(8,128)S(1)} %get-tuple-element.43, f32[8,34,258]{2,1,0:T(8,128)S(1)} %get-tuple-element.44, f32[8,34,258]{2,1,0:T(8,128)S(1)} %get-tuple-element.42, f32[32,256]{1,0:T(8,128)S(1)} %copy-done.9, ...), kind=kLoop, calls=%fused_computation.253 | loop fusion | flops 1441792 | bytes 3833856 | tf_op jit(solution)/shard_map/div | solution.py:125
  40.4 0.9 fusion.122
  41.5 1.1 %pad_maximum_fusion.2 = (f32[2,8,32,256]{3,2,1,0:T(8,128)S(1)}, f32[2,8,32,256]{3,2,1,0:T(8,128)}, f32[2,8,32,256]{3,2,1,0:T(8,128)S(1)}, f32[2,8,32,256]{3,2,1,0:T(8,128)S(1)}) fusion(f32[1,8,32,256]{3,2,1,0:T(8,128)S(1)} %bitcast.154, f32[1,8,32,256]{3,2,1,0:T(8,128)S(1)} %bitcast.157, f32[1,8,32,256]{3,2,1,0:T(8,128)S(1)} %bitcast.152, ...), kind=kLoop, calls=%fused_computation.29 | loop fusion | flops 1179648 | bytes 3670016 | tf_op jit(solution)/shard_map/stack | solution.py:136
  42.7 3.2 %collective-permute-start.8 = (f32[16,32,1]{2,1,0:T(8,128)S(1)}, f32[16,32,1]{2,1,0:T(8,128)S(1)}, u32[]{:S(2)}, u32[]{:S(2)}) collective-permute-start(f32[16,32,1]{2,1,0:T(8,128)S(1)} %get-tuple-element.57), channel_id=1, source_target_pairs={{8,0},{16,8},{24,16},{0,24},{9,1},{17,9},{25,17},{1,25},{10,2},{18... | collective-permute-start | bytes 6152 | tf_op jit(solution)/shard_map/ppermute | solution.py:23
  46.0 3.0 %collective-permute-start.12 = (f32[16,32,1]{2,1,0:T(8,128)S(1)}, f32[16,32,1]{2,1,0:T(8,128)S(1)}, u32[]{:S(2)}, u32[]{:S(2)}) collective-permute-start(f32[16,32,1]{2,1,0:T(8,128)S(1)} %get-tuple-element.63), channel_id=1, source_target_pairs={{8,0},{16,8},{24,16},{0,24},{9,1},{17,9},{25,17},{1,25},{10,2},{18... | collective-permute-start | bytes 6152 | tf_op jit(solution)/shard_map/ppermute | solution.py:23
  49.1 3.0 %collective-permute-start.16 = (f32[16,32,1]{2,1,0:T(8,128)S(1)}, f32[16,32,1]{2,1,0:T(8,128)S(1)}, u32[]{:S(2)}, u32[]{:S(2)}) collective-permute-start(f32[16,32,1]{2,1,0:T(8,128)S(1)} %get-tuple-element.65), channel_id=1, source_target_pairs={{8,0},{16,8},{24,16},{0,24},{9,1},{17,9},{25,17},{1,25},{10,2},{18... | collective-permute-start | bytes 6152 | tf_op jit(solution)/shard_map/ppermute | solution.py:23
  52.3 0.6 copy-done.17
  52.8 1.7 %fusion.26 = f32[8,32,256]{2,1,0:T(8,128)} fusion(f32[8,34,258]{2,1,0:T(8,128)S(1)} %get-tuple-element.40, f32[8,34,258]{2,1,0:T(8,128)S(1)} %get-tuple-element.41, f32[8,34,258]{2,1,0:T(8,128)S(1)} %get-tuple-element.39, f32[8,34,258]{2,1,0:T(8,128)S(1)} %get-tuple-element.103, f32[8,34,258]{2,1,0:T(8,128)S(1)} %get-tuple-element.102, ...), kind=kLoop, calls=%fused_computation.86 | loop fusion | flops 1572864 | bytes 5013504 | tf_op jit(solution)/shard_map/add | solution.py:169
  55.0 4.2 %collective-permute-done.9 = f32[16,32,1]{2,1,0:T(8,128)S(1)} collective-permute-done((f32[16,32,1]{2,1,0:T(8,128)S(1)}, f32[16,32,1]{2,1,0:T(8,128)S(1)}, u32[]{:S(2)}, u32[]{:S(2)}) %collective-permute-start.9) | collective-permute-done | bytes 2080 | tf_op jit(solution)/shard_map/ppermute | solution.py:21
  59.4 4.4 %collective-permute-done.12 = f32[16,32,1]{2,1,0:T(8,128)S(1)} collective-permute-done((f32[16,32,1]{2,1,0:T(8,128)S(1)}, f32[16,32,1]{2,1,0:T(8,128)S(1)}, u32[]{:S(2)}, u32[]{:S(2)}) %collective-permute-start.12) | collective-permute-done | bytes 2080 | tf_op jit(solution)/shard_map/ppermute | solution.py:23
  63.8 2.5 %collective-permute-start.11 = (f32[16,1,258]{2,1,0:T(1,128)S(1)}, f32[16,1,258]{2,1,0:T(1,128)S(1)}, u32[]{:S(2)}, u32[]{:S(2)}) collective-permute-start(f32[16,1,258]{2,1,0:T(1,128)S(1)} %get-tuple-element.52), channel_id=1, source_target_pairs={{1,0},{2,1},{3,2},{4,3},{5,4},{6,5},{7,6},{0,7},{9,8},{10,9},{11,1... | collective-permute-start | bytes 49544 | tf_op jit(solution)/shard_map/ppermute | solution.py:23
  66.3 4.1 %collective-permute-done.13 = f32[16,32,1]{2,1,0:T(8,128)S(1)} collective-permute-done((f32[16,32,1]{2,1,0:T(8,128)S(1)}, f32[16,32,1]{2,1,0:T(8,128)S(1)}, u32[]{:S(2)}, u32[]{:S(2)}) %collective-permute-start.13) | collective-permute-done | bytes 2080 | tf_op jit(solution)/shard_map/ppermute | solution.py:21
  70.7 4.4 %collective-permute-done.16 = f32[16,32,1]{2,1,0:T(8,128)S(1)} collective-permute-done((f32[16,32,1]{2,1,0:T(8,128)S(1)}, f32[16,32,1]{2,1,0:T(8,128)S(1)}, u32[]{:S(2)}, u32[]{:S(2)}) %collective-permute-start.16) | collective-permute-done | bytes 2080 | tf_op jit(solution)/shard_map/ppermute | solution.py:23
  75.0 2.5 %collective-permute-start.15 = (f32[16,1,258]{2,1,0:T(1,128)S(1)}, f32[16,1,258]{2,1,0:T(1,128)S(1)}, u32[]{:S(2)}, u32[]{:S(2)}) collective-permute-start(f32[16,1,258]{2,1,0:T(1,128)S(1)} %get-tuple-element.54), channel_id=1, source_target_pairs={{1,0},{2,1},{3,2},{4,3},{5,4},{6,5},{7,6},{0,7},{9,8},{10,9},{11,1... | collective-permute-start | bytes 49544 | tf_op jit(solution)/shard_map/ppermute | solution.py:23
  77.5 1.3 %collective-permute-done.17 = f32[16,32,1]{2,1,0:T(8,128)S(1)} collective-permute-done((f32[16,32,1]{2,1,0:T(8,128)S(1)}, f32[16,32,1]{2,1,0:T(8,128)S(1)}, u32[]{:S(2)}, u32[]{:S(2)}) %collective-permute-start.17) | collective-permute-done | bytes 2080 | tf_op jit(solution)/shard_map/ppermute | solution.py:21
  79.1 3.5 %collective-permute-start.19 = (f32[16,1,258]{2,1,0:T(1,128)S(1)}, f32[16,1,258]{2,1,0:T(1,128)S(1)}, u32[]{:S(2)}, u32[]{:S(2)}) collective-permute-start(f32[16,1,258]{2,1,0:T(1,128)S(1)} %get-tuple-element.56), channel_id=1, source_target_pairs={{1,0},{2,1},{3,2},{4,3},{5,4},{6,5},{7,6},{0,7},{9,8},{10,9},{11,1... | collective-permute-start | bytes 49544 | tf_op jit(solution)/shard_map/ppermute | solution.py:23
  83.2 0.9 collective-permute-done.18
  84.1 0.5 fusion.6
  84.7 3.6 %collective-permute-start.24 = (f32[8,1,257]{2,1,0:T(1,128)S(1)}, f32[8,1,257]{2,1,0:T(1,128)S(1)}, u32[]{:S(2)}, u32[]{:S(2)}) collective-permute-start(f32[8,1,257]{2,1,0:T(1,128)S(1)} %get-tuple-element.68), channel_id=1, source_target_pairs={{1,0},{2,1},{3,2},{4,3},{5,4},{6,5},{7,6},{0,7},{9,8},{10,9},{11,1... | collective-permute-start | bytes 24680 | tf_op jit(solution)/shard_map/ppermute | solution.py:23
  88.2 0.5 fusion.14
  89.6 1.1 %fusion.45 = (f32[1,8,32,256]{3,2,1,0:T(8,128)S(1)}, f32[1,8,32,256]{3,2,1,0:T(8,128)S(1)}, f32[8,32,256]{2,1,0:T(8,128)}) fusion(f32[8,1,257]{2,1,0:T(1,128)S(1)} %collective-permute-done.24, f32[8,32,257]{2,1,0:T(8,128)S(1)} %fusion.6, f32[3,8,34,258]{3,2,1,0:T(8,128)S(1)} %get-tuple-element.24, f32[8,32,256]{2,1,0:T(8,128)S(1)} %fusion.104, ...), kind=kLoop, calls=%fused_computation.113 | loop fusion | flops 1572864 | bytes 4427776 | tf_op jit(solution)/shard_map/stack | solution.py:161
  92.3 1.5 %collective-permute-done.23 = f32[8,1,257]{2,1,0:T(1,128)S(1)} collective-permute-done((f32[8,1,257]{2,1,0:T(1,128)S(1)}, f32[8,1,257]{2,1,0:T(1,128)S(1)}, u32[]{:S(2)}, u32[]{:S(2)}) %collective-permute-start.23) | collective-permute-done | bytes 8256 | tf_op jit(solution)/shard_map/ppermute | solution.py:21
  93.8 0.8 collective-permute-done.25
  94.6 0.6 fusion.32
  95.1 1.1 %fusion = f32[3,8,32,256]{3,2,1,0:T(8,128)} fusion(f32[1,8,32,256]{3,2,1,0:T(8,128)S(1)} %fusion.74, f32[1,8,32,256]{3,2,1,0:T(8,128)S(1)} %get-tuple-element.30, f32[1,8,32,256]{3,2,1,0:T(8,128)S(1)} %get-tuple-element.29, f32[1,8,32,256]{3,2,1,0:T(8,128)S(1)} %get-tuple-element.101, f32[1,8,32,256]{3,2,1,0:T(8,128)S(1)} %get-tuple-element.28, ...), kind=kLoop, calls=%fused_computation.8 | loop fusion | flops 2359296 | bytes 3145728 | tf_op jit(solution)/shard_map/add | solution.py:171
  (89 shorter events, 7.4 us)
Async XLA Ops:
  2.5 10.7 %collective-permute-start.4 = (f32[6,32,1]{2,1,0:T(8,128)S(1)}, f32[6,32,1]{2,1,0:T(8,128)S(1)}, u32[]{:S(2)}, u32[]{:S(2)}) collective-permute-start(f32[6,32,1]{2,1,0:T(8,128)S(1)} %get-tuple-element.84), channel_id=1, source_target_pairs={{0,8},{8,16},{16,24},{24,0},{1,9},{9,17},{17,25},{25,1},{2,10},{10... | collective-permute-start | bytes 2312 | tf_op jit(solution)/shard_map/ppermute | solution.py:21
  5.5 7.7 %collective-permute-start.5 = (f32[6,32,1]{2,1,0:T(8,128)S(1)}, f32[6,32,1]{2,1,0:T(8,128)S(1)}, u32[]{:S(2)}, u32[]{:S(2)}) collective-permute-start(f32[6,32,1]{2,1,0:T(8,128)S(1)} %get-tuple-element.85), channel_id=1, source_target_pairs={{8,0},{16,8},{24,16},{0,24},{9,1},{17,9},{25,17},{1,25},{10,2},{18... | collective-permute-start | bytes 2312 | tf_op jit(solution)/shard_map/ppermute | solution.py:23
  8.6 3.3 %copy-start.6 = (f32[2,3,32,256]{3,2,1,0:T(8,128)S(1)}, f32[2,3,32,256]{3,2,1,0:T(8,128)}, u32[]{:S(2)}) copy-start(f32[2,3,32,256]{3,2,1,0:T(8,128)} %param.16) | copy-start | bytes 589828
  8.6 4.0 %copy-start.16 = (f32[2,32,256]{2,1,0:T(8,128)S(1)}, f32[2,32,256]{2,1,0:T(8,128)}, u32[]{:S(2)}) copy-start(f32[2,32,256]{2,1,0:T(8,128)} %param.17) | copy-start | bytes 196612
  8.6 4.6 %copy-start.2 = (f32[3,32,256]{2,1,0:T(8,128)S(1)}, f32[3,32,256]{2,1,0:T(8,128)}, u32[]{:S(2)}) copy-start(f32[3,32,256]{2,1,0:T(8,128)} %param.13) | copy-start | bytes 294916
  9.3 11.0 %collective-permute-start.1 = (f32[64,32,1]{0,1,2:T(8,128)S(1)}, f32[64,32,1]{0,1,2:T(8,128)}, u32[]{:S(2)}, u32[]{:S(2)}) collective-permute-start(f32[64,32,1]{0,1,2:T(8,128)S(1)} %copy.38), channel_id=1, source_target_pairs={{8,0},{16,8},{24,16},{0,24},{9,1},{17,9},{25,17},{1,25},{10,2},{18... | collective-permute-start | bytes 24584 | tf_op jit(solution)/shard_map/ppermute | solution.py:23
  11.8 7.5 %collective-permute-start = (f32[64,32,1]{0,1,2:T(8,128)S(1)}, f32[64,32,1]{0,1,2:T(8,128)S(1)}, u32[]{:S(2)}, u32[]{:S(2)}) collective-permute-start(f32[64,32,1]{0,1,2:T(8,128)S(1)} %copy.37), channel_id=1, source_target_pairs={{0,8},{8,16},{16,24},{24,0},{1,9},{9,17},{17,25},{25,1},{2,10},{10... | collective-permute-start | bytes 24584 | tf_op jit(solution)/shard_map/ppermute | solution.py:21
  13.4 4.9 %collective-permute-start.6 = (f32[6,1,258]{2,1,0:T(1,128)S(1)}, f32[6,1,258]{2,1,0:T(1,128)S(1)}, u32[]{:S(2)}, u32[]{:S(2)}) collective-permute-start(f32[6,1,258]{2,1,0:T(1,128)S(1)} %get-tuple-element.74), channel_id=1, source_target_pairs={{0,1},{1,2},{2,3},{3,4},{4,5},{5,6},{6,7},{7,0},{8,9},{9,10},{10,1... | collective-permute-start | bytes 18584 | tf_op jit(solution)/shard_map/ppermute | solution.py:21
  13.5 4.9 %collective-permute-start.7 = (f32[6,1,258]{2,1,0:T(1,128)S(1)}, f32[6,1,258]{2,1,0:T(1,128)S(1)}, u32[]{:S(2)}, u32[]{:S(2)}) collective-permute-start(f32[6,1,258]{2,1,0:T(1,128)S(1)} %get-tuple-element.75), channel_id=1, source_target_pairs={{1,0},{2,1},{3,2},{4,3},{5,4},{6,5},{7,6},{0,7},{9,8},{10,9},{11,1... | collective-permute-start | bytes 18584 | tf_op jit(solution)/shard_map/ppermute | solution.py:23
  17.6 4.4 %copy-start = (f32[3,8,32,256]{3,2,1,0:T(8,128)S(1)}, f32[3,8,32,256]{3,2,1,0:T(8,128)}, u32[]{:S(2)}) copy-start(f32[3,8,32,256]{3,2,1,0:T(8,128)} %param.11) | copy-start | bytes 2359300
  17.6 4.4 %copy-start.3 = (f32[8,32,256]{2,1,0:T(8,128)S(1)}, f32[8,32,256]{2,1,0:T(8,128)}, u32[]{:S(2)}) copy-start(f32[8,32,256]{2,1,0:T(8,128)} %param.12) | copy-start | bytes 786436
  17.6 4.4 %copy-start.4 = (f32[8,32,256]{2,1,0:T(8,128)S(1)}, f32[8,32,256]{2,1,0:T(8,128)}, u32[]{:S(2)}) copy-start(f32[8,32,256]{2,1,0:T(8,128)} %param.10) | copy-start | bytes 786436
  22.0 5.6 %copy-start.5 = (f32[6,34,258]{2,1,0:T(8,128)S(1)}, f32[6,34,258]{2,1,0:T(8,128)}, u32[]{:S(2)}) copy-start(f32[6,34,258]{2,1,0:T(8,128)} %pad_maximum_fusion.11) | copy-start | bytes 631588
  22.0 7.8 %copy-start.1 = (f32[3,8,32,256]{3,2,1,0:T(8,128)S(1)}, f32[3,8,32,256]{3,2,1,0:T(8,128)}, u32[]{:S(2)}) copy-start(f32[3,8,32,256]{3,2,1,0:T(8,128)} %param.9) | copy-start | bytes 2359300
  23.8 6.0 %collective-permute-start.2 = (f32[64,1,258]{2,1,0:T(1,128)S(1)}, f32[64,1,258]{2,1,0:T(1,128)S(1)}, u32[]{:S(2)}, u32[]{:S(2)}) collective-permute-start(f32[64,1,258]{2,1,0:T(1,128)S(1)} %get-tuple-element.14), channel_id=1, source_target_pairs={{0,1},{1,2},{2,3},{3,4},{4,5},{5,6},{6,7},{7,0},{8,9},{9,10},{10,1... | collective-permute-start | bytes 198152 | tf_op jit(solution)/shard_map/ppermute | solution.py:21
  24.1 5.7 %collective-permute-start.3 = (f32[64,1,258]{2,1,0:T(1,128)S(1)}, f32[64,1,258]{2,1,0:T(1,128)S(1)}, u32[]{:S(2)}, u32[]{:S(2)}) collective-permute-start(f32[64,1,258]{2,1,0:T(1,128)S(1)} %get-tuple-element.15), channel_id=1, source_target_pairs={{1,0},{2,1},{3,2},{4,3},{5,4},{6,5},{7,6},{0,7},{9,8},{10,9},{11,1... | collective-permute-start | bytes 198152 | tf_op jit(solution)/shard_map/ppermute | solution.py:23
  37.6 0.8 copy-start.7
  37.6 0.8 copy-start.12
  37.6 0.8 copy-start.13
  37.8 1.1 %copy-start.8 = (f32[32,256]{1,0:T(8,128)S(1)}, f32[32,256]{1,0:T(8,128)}, u32[]{:S(2)}) copy-start(f32[32,256]{1,0:T(8,128)} %get-tuple-element.78) | copy-start | bytes 98308
  37.8 1.1 %copy-start.9 = (f32[32,256]{1,0:T(8,128)S(1)}, f32[32,256]{1,0:T(8,128)}, u32[]{:S(2)}) copy-start(f32[32,256]{1,0:T(8,128)} %get-tuple-element.80) | copy-start | bytes 98308
  37.8 1.1 %copy-start.10 = (f32[32,256]{1,0:T(8,128)S(1)}, f32[32,256]{1,0:T(8,128)}, u32[]{:S(2)}) copy-start(f32[32,256]{1,0:T(8,128)} %get-tuple-element.81) | copy-start | bytes 98308
  37.8 1.1 %copy-start.14 = (f32[32,256]{1,0:T(8,128)S(1)}, f32[32,256]{1,0:T(8,128)}, u32[]{:S(2)}) copy-start(f32[32,256]{1,0:T(8,128)} %get-tuple-element.98) | copy-start | bytes 98308
  37.8 1.1 %copy-start.15 = (f32[32,256]{1,0:T(8,128)S(1)}, f32[32,256]{1,0:T(8,128)}, u32[]{:S(2)}) copy-start(f32[32,256]{1,0:T(8,128)} %get-tuple-element.109) | copy-start | bytes 98308
  42.7 11.8 %collective-permute-start.8 = (f32[16,32,1]{2,1,0:T(8,128)S(1)}, f32[16,32,1]{2,1,0:T(8,128)S(1)}, u32[]{:S(2)}, u32[]{:S(2)}) collective-permute-start(f32[16,32,1]{2,1,0:T(8,128)S(1)} %get-tuple-element.57), channel_id=1, source_target_pairs={{8,0},{16,8},{24,16},{0,24},{9,1},{17,9},{25,17},{1,25},{10,2},{18... | collective-permute-start | bytes 6152 | tf_op jit(solution)/shard_map/ppermute | solution.py:23
  45.9 13.3 %collective-permute-start.9 = (f32[16,32,1]{2,1,0:T(8,128)S(1)}, f32[16,32,1]{2,1,0:T(8,128)S(1)}, u32[]{:S(2)}, u32[]{:S(2)}) collective-permute-start(f32[16,32,1]{2,1,0:T(8,128)S(1)} %get-tuple-element.58), channel_id=1, source_target_pairs={{0,8},{8,16},{16,24},{24,0},{1,9},{9,17},{17,25},{25,1},{2,10},{10... | collective-permute-start | bytes 6152 | tf_op jit(solution)/shard_map/ppermute | solution.py:21
  46.0 17.8 %collective-permute-start.12 = (f32[16,32,1]{2,1,0:T(8,128)S(1)}, f32[16,32,1]{2,1,0:T(8,128)S(1)}, u32[]{:S(2)}, u32[]{:S(2)}) collective-permute-start(f32[16,32,1]{2,1,0:T(8,128)S(1)} %get-tuple-element.63), channel_id=1, source_target_pairs={{8,0},{16,8},{24,16},{0,24},{9,1},{17,9},{25,17},{1,25},{10,2},{18... | collective-permute-start | bytes 6152 | tf_op jit(solution)/shard_map/ppermute | solution.py:23
  49.0 21.4 %collective-permute-start.13 = (f32[16,32,1]{2,1,0:T(8,128)S(1)}, f32[16,32,1]{2,1,0:T(8,128)S(1)}, u32[]{:S(2)}, u32[]{:S(2)}) collective-permute-start(f32[16,32,1]{2,1,0:T(8,128)S(1)} %get-tuple-element.64), channel_id=1, source_target_pairs={{0,8},{8,16},{16,24},{24,0},{1,9},{9,17},{17,25},{25,1},{2,10},{10... | collective-permute-start | bytes 6152 | tf_op jit(solution)/shard_map/ppermute | solution.py:21
  49.1 25.9 %collective-permute-start.16 = (f32[16,32,1]{2,1,0:T(8,128)S(1)}, f32[16,32,1]{2,1,0:T(8,128)S(1)}, u32[]{:S(2)}, u32[]{:S(2)}) collective-permute-start(f32[16,32,1]{2,1,0:T(8,128)S(1)} %get-tuple-element.65), channel_id=1, source_target_pairs={{8,0},{16,8},{24,16},{0,24},{9,1},{17,9},{25,17},{1,25},{10,2},{18... | collective-permute-start | bytes 6152 | tf_op jit(solution)/shard_map/ppermute | solution.py:23
  52.1 0.8 copy-start.17
  54.5 24.3 %collective-permute-start.17 = (f32[16,32,1]{2,1,0:T(8,128)S(1)}, f32[16,32,1]{2,1,0:T(8,128)S(1)}, u32[]{:S(2)}, u32[]{:S(2)}) collective-permute-start(f32[16,32,1]{2,1,0:T(8,128)S(1)} %get-tuple-element.66), channel_id=1, source_target_pairs={{0,8},{8,16},{16,24},{24,0},{1,9},{9,17},{17,25},{25,1},{2,10},{10... | collective-permute-start | bytes 6152 | tf_op jit(solution)/shard_map/ppermute | solution.py:21
  59.4 19.7 %collective-permute-start.10 = (f32[16,1,258]{2,1,0:T(1,128)S(1)}, f32[16,1,258]{2,1,0:T(1,128)S(1)}, u32[]{:S(2)}, u32[]{:S(2)}) collective-permute-start(f32[16,1,258]{2,1,0:T(1,128)S(1)} %get-tuple-element.51), channel_id=1, source_target_pairs={{0,1},{1,2},{2,3},{3,4},{4,5},{5,6},{6,7},{7,0},{8,9},{9,10},{10,1... | collective-permute-start | bytes 49544 | tf_op jit(solution)/shard_map/ppermute | solution.py:21
  63.8 18.8 %collective-permute-start.11 = (f32[16,1,258]{2,1,0:T(1,128)S(1)}, f32[16,1,258]{2,1,0:T(1,128)S(1)}, u32[]{:S(2)}, u32[]{:S(2)}) collective-permute-start(f32[16,1,258]{2,1,0:T(1,128)S(1)} %get-tuple-element.52), channel_id=1, source_target_pairs={{1,0},{2,1},{3,2},{4,3},{5,4},{6,5},{7,6},{0,7},{9,8},{10,9},{11,1... | collective-permute-start | bytes 49544 | tf_op jit(solution)/shard_map/ppermute | solution.py:23
  70.6 17.6 %collective-permute-start.14 = (f32[16,1,258]{2,1,0:T(1,128)S(1)}, f32[16,1,258]{2,1,0:T(1,128)S(1)}, u32[]{:S(2)}, u32[]{:S(2)}) collective-permute-start(f32[16,1,258]{2,1,0:T(1,128)S(1)} %get-tuple-element.53), channel_id=1, source_target_pairs={{0,1},{1,2},{2,3},{3,4},{4,5},{5,6},{6,7},{7,0},{8,9},{9,10},{10,1... | collective-permute-start | bytes 49544 | tf_op jit(solution)/shard_map/ppermute | solution.py:21
  75.0 13.2 %collective-permute-start.15 = (f32[16,1,258]{2,1,0:T(1,128)S(1)}, f32[16,1,258]{2,1,0:T(1,128)S(1)}, u32[]{:S(2)}, u32[]{:S(2)}) collective-permute-start(f32[16,1,258]{2,1,0:T(1,128)S(1)} %get-tuple-element.54), channel_id=1, source_target_pairs={{1,0},{2,1},{3,2},{4,3},{5,4},{6,5},{7,6},{0,7},{9,8},{10,9},{11,1... | collective-permute-start | bytes 49544 | tf_op jit(solution)/shard_map/ppermute | solution.py:23
  79.0 5.1 %collective-permute-start.18 = (f32[16,1,258]{2,1,0:T(1,128)S(1)}, f32[16,1,258]{2,1,0:T(1,128)S(1)}, u32[]{:S(2)}, u32[]{:S(2)}) collective-permute-start(f32[16,1,258]{2,1,0:T(1,128)S(1)} %get-tuple-element.55), channel_id=1, source_target_pairs={{0,1},{1,2},{2,3},{3,4},{4,5},{5,6},{6,7},{7,0},{8,9},{9,10},{10,1... | collective-permute-start | bytes 49544 | tf_op jit(solution)/shard_map/ppermute | solution.py:21
  79.1 5.0 %collective-permute-start.19 = (f32[16,1,258]{2,1,0:T(1,128)S(1)}, f32[16,1,258]{2,1,0:T(1,128)S(1)}, u32[]{:S(2)}, u32[]{:S(2)}) collective-permute-start(f32[16,1,258]{2,1,0:T(1,128)S(1)} %get-tuple-element.56), channel_id=1, source_target_pairs={{1,0},{2,1},{3,2},{4,3},{5,4},{6,5},{7,6},{0,7},{9,8},{10,9},{11,1... | collective-permute-start | bytes 49544 | tf_op jit(solution)/shard_map/ppermute | solution.py:23
  83.1 7.6 %collective-permute-start.20 = (f32[8,1,257]{2,1,0:T(1,128)S(1)}, f32[8,1,257]{2,1,0:T(1,128)S(1)}, u32[]{:S(2)}, u32[]{:S(2)}) collective-permute-start(f32[8,1,257]{2,1,0:T(1,128)S(1)} %get-tuple-element.72), channel_id=1, source_target_pairs={{1,0},{2,1},{3,2},{4,3},{5,4},{6,5},{7,6},{0,7},{9,8},{10,9},{11,1... | collective-permute-start | bytes 24680 | tf_op jit(solution)/shard_map/ppermute | solution.py:23
  84.1 7.6 %collective-permute-start.21 = (f32[8,1,257]{2,1,0:T(1,128)S(1)}, f32[8,1,257]{2,1,0:T(1,128)S(1)}, u32[]{:S(2)}, u32[]{:S(2)}) collective-permute-start(f32[8,1,257]{2,1,0:T(1,128)S(1)} %get-tuple-element.73), channel_id=1, source_target_pairs={{0,1},{1,2},{2,3},{3,4},{4,5},{5,6},{6,7},{7,0},{8,9},{9,10},{10,1... | collective-permute-start | bytes 24680 | tf_op jit(solution)/shard_map/ppermute | solution.py:21
  84.7 5.0 %collective-permute-start.24 = (f32[8,1,257]{2,1,0:T(1,128)S(1)}, f32[8,1,257]{2,1,0:T(1,128)S(1)}, u32[]{:S(2)}, u32[]{:S(2)}) collective-permute-start(f32[8,1,257]{2,1,0:T(1,128)S(1)} %get-tuple-element.68), channel_id=1, source_target_pairs={{1,0},{2,1},{3,2},{4,3},{5,4},{6,5},{7,6},{0,7},{9,8},{10,9},{11,1... | collective-permute-start | bytes 24680 | tf_op jit(solution)/shard_map/ppermute | solution.py:23
  88.8 2.5 %collective-permute-start.22 = (f32[8,1,257]{2,1,0:T(1,128)S(1)}, f32[8,1,257]{2,1,0:T(1,128)S(1)}, u32[]{:S(2)}, u32[]{:S(2)}) collective-permute-start(f32[8,1,257]{2,1,0:T(1,128)S(1)} %get-tuple-element.70), channel_id=1, source_target_pairs={{1,0},{2,1},{3,2},{4,3},{5,4},{6,5},{7,6},{0,7},{9,8},{10,9},{11,1... | collective-permute-start | bytes 24680 | tf_op jit(solution)/shard_map/ppermute | solution.py:23
  88.9 5.0 %collective-permute-start.23 = (f32[8,1,257]{2,1,0:T(1,128)S(1)}, f32[8,1,257]{2,1,0:T(1,128)S(1)}, u32[]{:S(2)}, u32[]{:S(2)}) collective-permute-start(f32[8,1,257]{2,1,0:T(1,128)S(1)} %get-tuple-element.71), channel_id=1, source_target_pairs={{0,1},{1,2},{2,3},{3,4},{4,5},{5,6},{6,7},{7,0},{8,9},{9,10},{10,1... | collective-permute-start | bytes 24680 | tf_op jit(solution)/shard_map/ppermute | solution.py:21
  89.6 4.9 %collective-permute-start.25 = (f32[8,1,257]{2,1,0:T(1,128)S(1)}, f32[8,1,257]{2,1,0:T(1,128)S(1)}, u32[]{:S(2)}, u32[]{:S(2)}) collective-permute-start(f32[8,1,257]{2,1,0:T(1,128)S(1)} %get-tuple-element.69), channel_id=1, source_target_pairs={{0,1},{1,2},{2,3},{3,4},{4,5},{5,6},{6,7},{7,0},{8,9},{9,10},{10,1... | collective-permute-start | bytes 24680 | tf_op jit(solution)/shard_map/ppermute | solution.py:21
  91.2 0.8 copy-start.11
where the time goes:
time: 96.8 us; the launch traced here: 96.2 us
  starting transfers between devices  36 us (37%)
  other arithmetic  25.5 us (26%)
  waiting for transfers between devices  24.7 us (26%)
  local copies, waits for them, and re-layouts  8.85 us (9%)
  between operations  1.18 us (1%)
    ppermute x13, starting transfers between devices, with_halo(): lax.ppermute(head, axis, [((i + 1) % count, i) for i in range(count)])  31.4 us
    ppermute x13, waiting for transfers between devices, with_halo(): lax.ppermute(tail, axis, [(i, (i + 1) % count) for i in range(count)])  15.6 us
    ppermute x13, waiting for transfers between devices, with_halo(): lax.ppermute(head, axis, [((i + 1) % count, i) for i in range(count)])  9.08 us
    concatenate x2, other arithmetic, with_halo(): jnp.concatenate([lax.ppermute(tail, axis, [(i, (i + 1) % count) for i in...  7.06 us
    ppermute x13, starting transfers between devices, with_halo(): lax.ppermute(tail, axis, [(i, (i + 1) % count) for i in range(count)])  4.6 us
    another operation x5, other arithmetic, local(): jnp.stack([mean_zero - UPWIND_FACTOR * inner_velocity[0] * grad_zero, mea...  2.87 us
    slice x5, other arithmetic, with_halo(): lax.slice_in_dim(cells, cells.shape[dim] - width, cells.shape[dim], axis=...  2.45 us
  transfers between devices with their start and end apart: 26, of which 11 were waited for; matrix products, arithmetic and copies ran while one was open for 14% of the time, Pallas kernels for 0%

commit v1 on v0

v1 whole, which is shorter than its diff:
```python
import jax
import jax.numpy as jnp
from jax import lax
from jax.experimental import pallas as pl
from jax.experimental.pallas import tpu as pltpu
from jax.sharding import PartitionSpec as P

SUB = 8
LANE = 128
COMPS = 8
GEO = 14
LANE_STEP = 2 * COMPS
MESH = pl.DeviceIdType.MESH


def iotas():
    sub = lax.broadcasted_iota(jnp.int32, (SUB, LANE), 0)
    lane = lax.broadcasted_iota(jnp.int32, (SUB, LANE), 1)
    return sub, lane


def exchange_kernel(counts, *refs):
    (vel, th, vt, tt, cd, el, kite, cor) = refs[:8]
    (o_bot, o_top, o_right, o_left, o_br, o_tr, o_bl) = refs[8:15]
    bufs = refs[15:23]
    (p_bot, p_top, p_right, p_left) = refs[23:27]
    in_sem, send_sem, recv_sem = refs[27:30]
    ny, nx = counts
    py, px = lax.axis_index("py"), lax.axis_index("px")
    down, up = lax.rem(py + 1, ny), lax.rem(py + ny - 1, ny)
    right, left = lax.rem(px + 1, nx), lax.rem(px + nx - 1, nx)

    loads = [
        pltpu.make_async_copy(src, dst, in_sem.at[i])
        for i, (src, dst) in enumerate(zip((vel, th, vt, tt, cd, el, kite, cor), bufs))
    ]
    for i in (4, 5, 6, 7, 0, 1, 2, 3):
        loads[i].start()
    barrier = pltpu.get_barrier_semaphore()
    near = [
        (up, px), (down, px), (py, left), (py, right),
        (up, left), (up, right), (down, left), (down, right),
    ]
    for y, x in near:
        pl.semaphore_signal(barrier, inc=1, device_id={"py": y, "px": x}, device_id_type=MESH)

    b_vel, b_th, b_vt, b_tt, b_cd, b_el, b_kite, b_cor = bufs
    levels, rows, cols = b_th.shape
    nr, nc = rows // SUB, cols // LANE
    sub, lane = iotas()
    last = slice(cols - LANE, cols)

    def view(ref, *lead):
        return lambda r, c: ref[lead + (r, c)]

    def level_comps(l):
        return (
            [view(b_vel, k, l) for k in range(3)]
            + [view(b_th, l)]
            + [view(b_vt, k, l) for k in range(3)]
            + [view(b_tt, l)]
        )

    geo = (
        [view(b_cd, k) for k in range(3)]
        + [view(b_el, k) for k in range(3)]
        + [view(b_kite, v, k) for v in range(2) for k in range(3)]
        + [view(b_cor, v) for v in range(2)]
    )

    def pack_rows(comps, base):
        for g in range(0, len(comps), 4):
            for c in range(nc):
                cs = slice(c * LANE, (c + 1) * LANE)
                bot = top = jnp.zeros((SUB, LANE), jnp.float32)
                for q, f in enumerate(comps[g : g + 4]):
                    m = jnp.where(sub < 4, f(slice(0, SUB), cs), f(slice(rows - SUB, rows), cs))
                    m = pltpu.roll(m, 2 * q, 0) if q else m
                    bot = jnp.where((sub == 2 * q) | (sub == 2 * q + 1), m, bot)
                    t = (2 * q + 6) % SUB
                    top = jnp.where((sub == t) | (sub == t + 1), m, top)
                at = slice(base + 2 * g, base + 2 * g + SUB)
                p_bot[at, cs] = bot
                p_top[at, cs] = top

    def pack_cols(items, tile):
        for r in range(nr):
            rs = slice(r * SUB, (r + 1) * SUB)
            ra = la = jnp.zeros((SUB, LANE), jnp.float32)
            for s, f in items:
                m = jnp.where(lane < LANE // 2, f(rs, slice(0, LANE)), f(rs, last))
                m = pltpu.roll(m, s, 1) if s else m
                ra = jnp.where((lane == s) | (lane == s + 1), m, ra)
                la = jnp.where(lane == (s + LANE - 1) % LANE, m, la)
            cs = slice(tile * LANE, (tile + 1) * LANE)
            p_right[rs, cs] = ra
            p_left[rs, cs] = la

    for i in (4, 5, 6, 7):
        loads[i].wait()
    pack_rows(geo, levels * LANE_STEP)
    pack_cols([(2 * k, f) for k, f in enumerate(geo)], 1)
    for i in (0, 1, 2, 3):
        loads[i].wait()
    items = []
    for l in range(levels):
        comps = level_comps(l)
        items += [(l * LANE_STEP + 2 * k, f) for k, f in enumerate(comps)]
    pack_cols(items, 0)
    for l in range(levels):
        pack_rows(level_comps(l), l * LANE_STEP)

    pl.semaphore_wait(barrier, len(near))
    plan = [
        (p_bot, o_bot, (up, px)),
        (p_top, o_top, (down, px)),
        (p_right.at[rows - SUB : rows], o_tr, (down, left)),
        (p_right.at[0:SUB], o_br, (up, left)),
        (p_left.at[0:SUB], o_bl, (up, right)),
        (p_right, o_right, (py, left)),
        (p_left, o_left, (py, right)),
    ]
    copies = [
        pltpu.make_async_remote_copy(
            src_ref=src,
            dst_ref=dst,
            send_sem=send_sem.at[i],
            recv_sem=recv_sem.at[i],
            device_id={"py": y, "px": x},
            device_id_type=MESH,
        )
        for i, (src, dst, (y, x)) in enumerate(plan)
    ]
    for copy in copies:
        copy.start()
    for copy in copies:
        copy.wait()


def exchange(counts, vel, th, vt, tt, cd, el, kite, cor):
    levels, rows, cols = th.shape
    f32 = jnp.float32
    band = (levels * LANE_STEP + 32, cols)
    side = (rows, 2 * LANE)
    corner = (SUB, 2 * LANE)
    args = (vel, th, vt, tt, cd, el, kite, cor)
    outs = (band, band, side, side, corner, corner, corner)
    return pl.pallas_call(
        lambda *refs: exchange_kernel(counts, *refs),
        out_shape=[jax.ShapeDtypeStruct(s, f32) for s in outs],
        in_specs=[pl.BlockSpec(memory_space=pl.ANY)] * len(args),
        out_specs=[pl.BlockSpec(memory_space=pl.ANY)] * len(outs),
        scratch_shapes=[pltpu.VMEM(a.shape, f32) for a in args]
        + [pltpu.VMEM(s, f32) for s in (band, band, side, side)]
        + [
            pltpu.SemaphoreType.DMA((len(args),)),
            pltpu.SemaphoreType.DMA((len(outs),)),
            pltpu.SemaphoreType.DMA((len(outs),)),
        ],
        compiler_params=pltpu.CompilerParams(collective_id=0, has_side_effects=True),
        name="exchange",
    )(*args)


class Field:
    def __init__(self, grid, make):
        self.grid, self.make, self.memo = grid, make, {}

    def __call__(self, r, c):
        key = (r % self.grid[0], c % self.grid[1])
        if key not in self.memo:
            self.memo[key] = self.make(*key)
        return self.memo[key]


def step_kernel(
    vel, th, vt, tt, cd, el, kite, cor, area,
    bot, top, gbot, gtop, right, left, br, tr, bl,
    o_vert, o_kin, o_cell, o_edge, geo, scale,
):
    level = pl.program_id(0)
    rows, cols = area.shape
    nr, nc = rows // SUB, cols // LANE
    grid = (nr + 1, nc + 1)
    sub, lane = iotas()

    def at(r, c):
        return (slice(r * SUB, (r + 1) * SUB), slice(c * LANE, (c + 1) * LANE))

    def lift(fn, *fields):
        return Field(grid, lambda r, c: fn(*[f(r, c) for f in fields]))

    def row_shift(f, a):
        rolled = Field(grid, lambda r, c: pltpu.roll(f(r, c), (-a) % SUB, 0))
        if a == 1:
            return Field(grid, lambda r, c: jnp.where(sub < SUB - 1, rolled(r, c), rolled(r + 1, c)))
        return Field(grid, lambda r, c: jnp.where(sub > 0, rolled(r, c), rolled(r - 1, c)))

    def col_shift(f, b):
        rolled = Field(grid, lambda r, c: pltpu.roll(f(r, c), (-b) % LANE, 1))
        if b == 1:
            return Field(grid, lambda r, c: jnp.where(lane < LANE - 1, rolled(r, c), rolled(r, c + 1)))
        return Field(grid, lambda r, c: jnp.where(lane > 0, rolled(r, c), rolled(r, c - 1)))

    def extended(own, k, band_bot, band_top, side):
        q, g = k % 4, k // 4

        def make(r, c):
            if r < nr and c < nc:
                return own(*at(r, c))
            if c < nc:
                b, t = band_bot[at(g, c)], band_top[at(g, c)]
                m = jnp.where((sub == 2 * q) | (sub == 2 * q + 1), b, t)
                return pltpu.roll(m, (-2 * q) % SUB, 0) if q else m
            rt, lt = side(r)
            m = jnp.where((lane == 2 * k) | (lane == 2 * k + 1), rt, lt)
            return pltpu.roll(m, (-2 * k) % LANE, 1) if k else m

        return Field(grid, make)

    def side_of(tile, turn):
        cs = slice(tile * LANE, (tile + 1) * LANE)
        memo = {}

        def side(r):
            if r not in memo:
                if r < nr:
                    rs = slice(r * SUB, (r + 1) * SUB)
                    pair = right[rs, cs], left[rs, cs]
                else:
                    pair = jnp.where(sub < 4, br[:, cs], tr[:, cs]), bl[:, cs]
                memo[r] = tuple(turn(x) for x in pair)
            return memo[r]

        return side

    def view(ref, *lead):
        return lambda r, c: ref[lead + (r, c)]

    @pl.when(level == 0)
    def _():
        side = side_of(1, lambda x: x)
        owns = (
            [view(cd, k) for k in range(3)]
            + [view(el, k) for k in range(3)]
            + [view(kite, v, k) for v in range(2) for k in range(3)]
            + [view(cor, v) for v in range(2)]
        )
        f = [extended(own, k, gbot, gtop, side) for k, own in enumerate(owns)]
        for r in range(nr + 1):
            for c in range(nc + 1):
                for k in range(3):
                    geo[(k,) + at(r, c)] = f[k](r, c)
                    geo[(3 + k,) + at(r, c)] = 0.25 * f[k](r, c) * f[3 + k](r, c)
                for k in range(6):
                    geo[(6 + k,) + at(r, c)] = f[6 + k](r, c)
                for v in range(2):
                    t = f[6 + 3 * v](r, c) + f[7 + 3 * v](r, c) + f[8 + 3 * v](r, c)
                    geo[(12 + v,) + at(r, c)] = f[12 + v](r, c) * t
                if r < nr and c < nc:
                    for k in range(3):
                        scale[(k,) + at(r, c)] = (-0.5 / 36.0) / f[k](r, c)
                    scale[(3,) + at(r, c)] = 1.0 / area[at(r, c)]

    turn_by = lax.rem(LANE - level * LANE_STEP, LANE)
    side = side_of(0, lambda x: pltpu.roll(x, turn_by, 1))
    owns = (
        [view(vel, k, 0) for k in range(3)]
        + [view(th, 0)]
        + [view(vt, k, 0) for k in range(3)]
        + [view(tt, 0)]
    )
    x = [extended(own, k, bot, top, side) for k, own in enumerate(owns)]
    v, h, t, g = x[0:3], x[3], x[4:7], x[7]

    def geo_tile(k):
        return lambda r, c: geo[(k,) + at(r % grid[0], c % grid[1])]

    dist = [geo_tile(k) for k in range(3)]
    ew = [geo_tile(3 + k) for k in range(3)]
    kt = [geo_tile(6 + k) for k in range(6)]
    ct = [geo_tile(12 + k) for k in range(2)]

    def parts(vv, hh):
        flux = [lift(lambda a, b: a * b, vv[k], dist[k]) for k in range(3)]
        c0 = lift(lambda a, b, c: a + b - c, flux[0], row_shift(flux[2], 1), flux[1])
        c1 = lift(
            lambda a, b, c: a - b - c, flux[1], flux[2], col_shift(row_shift(flux[0], -1), 1)
        )
        hc = col_shift(hh, 1)
        hr = row_shift(hh, 1)
        hd = row_shift(hc, -1)
        mix = lambda a, b, c, p, q, s: a * p + b * q + c * s
        h0 = lift(mix, kt[0], kt[1], kt[2], hh, hr, hc)
        h1 = lift(mix, kt[3], kt[4], kt[5], hh, hc, hd)
        return (c0, c1), (h0, h1)

    cv, hv = parts(v, h)
    cw, hw = parts(t, g)

    def potential(k):
        def make(r, c):
            a0 = ct[k](r, c) + cv[k](r, c)
            a1 = cw[k](r, c)
            b0 = hv[k](r, c)
            b1 = hw[k](r, c)
            first = a0 / b0
            mid = (a0 + 0.5 * a1) / (b0 + 0.5 * b1)
            end = (a0 + a1) / (b0 + b1)
            late = 2.0 * mid + end
            return first + 2.0 * mid + late, late

        both = Field(grid, make)
        return Field(grid, lambda r, c: both(r, c)[0]), Field(grid, lambda r, c: both(r, c)[1])

    p0, q0 = potential(0)
    p1, q1 = potential(1)
    add = lambda a, b: a + b
    add3 = lambda a, b, c: a + b + c

    def cell(f0, f1):
        f0_up = row_shift(f0, -1)
        f1_down = row_shift(f1, 1)
        pair = lift(add, f0, f1)
        return lift(add3, pair, f0_up, col_shift(lift(add, pair, f1_down), -1)), f0_up, f1_down, pair

    cc, p0_up, p1_down, pair = cell(p0, p1)
    dd = cell(q0, q1)[0]
    p1_low = col_shift(p1_down, -1)

    def neighbours(f):
        fc = col_shift(f, 1)
        return row_shift(f, 1), fc, row_shift(fc, -1)

    cn, dn = neighbours(cc), neighbours(dd)
    ends = [lift(add, p0, p1_low), pair, lift(add, p1, p0_up)]
    en = [
        lift(lambda w, a, b: w * (a * (a + b) + (1.0 / 3.0) * (b * b)), ew[k], v[k], t[k])
        for k in range(3)
    ]
    e_up = row_shift(en[0], -1)
    e_low = col_shift(lift(add, en[1], row_shift(en[2], 1)), -1)

    for r in range(nr):
        for c in range(nc):
            p = at(r, c)
            o_vert[(0, 0) + p] = p0(r, c) * (1.0 / 6.0)
            o_vert[(1, 0) + p] = p1(r, c) * (1.0 / 6.0)
            total = en[0](r, c) + en[1](r, c) + en[2](r, c) + e_up(r, c) + e_low(r, c)
            o_kin[(0,) + p] = total * scale[(3,) + p]
            o_cell[(0,) + p] = cc(r, c) * (1.0 / 36.0)
            for k in range(3):
                slope = v[k](r, c) * (cn[k](r, c) - cc(r, c)) + t[k](r, c) * (dn[k](r, c) - dd(r, c))
                o_edge[(k, 0) + p] = ends[k](r, c) * (1.0 / 12.0) + scale[(k,) + p] * slope


def local(counts, vel, th, vt, tt, cd, el, area, kite, cor):
    bot, top, right, left, br, tr, bl = exchange(counts, vel, th, vt, tt, cd, el, kite, cor)
    levels, rows, cols = th.shape
    f32 = jnp.float32
    whole = lambda a: pl.BlockSpec(a.shape, lambda l: (0,) * a.ndim)
    three = pl.BlockSpec((3, 1, rows, cols), lambda l: (0, l, 0, 0))
    two = pl.BlockSpec((2, 1, rows, cols), lambda l: (0, l, 0, 0))
    one = pl.BlockSpec((1, rows, cols), lambda l: (l, 0, 0))
    band = pl.BlockSpec((LANE_STEP, cols), lambda l: (l, 0))
    gband = pl.BlockSpec((32, cols), lambda l: (levels * LANE_STEP // 32, 0))
    return pl.pallas_call(
        step_kernel,
        grid=(levels,),
        out_shape=[
            jax.ShapeDtypeStruct((2, levels, rows, cols), f32),
            jax.ShapeDtypeStruct((levels, rows, cols), f32),
            jax.ShapeDtypeStruct((levels, rows, cols), f32),
            jax.ShapeDtypeStruct((3, levels, rows, cols), f32),
        ],
        in_specs=[
            three, one, three, one, whole(cd), whole(el), whole(kite), whole(cor), whole(area),
            band, band, gband, gband, whole(right), whole(left), whole(br), whole(tr), whole(bl),
        ],
        out_specs=[two, one, one, three],
        scratch_shapes=[
            pltpu.VMEM((GEO, rows + SUB, cols + LANE), f32),
            pltpu.VMEM((4, rows, cols), f32),
        ],
        name="step",
    )(vel, th, vt, tt, cd, el, kite, cor, area, bot, top, bot, top, right, left, br, tr, bl)


def solution(mesh):
    counts = (mesh.shape["py"], mesh.shape["px"])
    p4, p3 = P(None, None, "py", "px"), P(None, "py", "px")
    return jax.shard_map(
        lambda *args: local(counts, *args),
        mesh=mesh,
        in_specs=(p4, p3, p4, p3, p3, p3, P("py", "px"), p4, p3),
        out_specs=(p4, p3, p3, p4),
        check_vma=False,
    )
```

time: 96.8 us -> 21 us (0.22)
  starting transfers between devices: 36 us -> 0 us
  other arithmetic: 25.5 us -> 0 us
  waiting for transfers between devices: 24.7 us -> 0 us
  Pallas kernels: 0 us -> 20 us
  local copies, waits for them, and re-layouts: 8.85 us -> 0 us
    ppermute x26 -> x0, starting transfers between devices: 36 us -> none  [the longest x13 31.4 us: with_halo(): lax.ppermute(head, axis, [((i + 1) % count, i) for i in range(count)])]
    ppermute x26 -> x0, waiting for transfers between devices: 24.7 us -> none  [the longest x13 15.6 us: with_halo(): lax.ppermute(tail, axis, [(i, (i + 1) % count) for i in range(count)])]
    pallas_call x0 -> x2, Pallas kernels: none -> 20 us  [the longest x1 12 us: exchange(): pl.pallas_call(lambda *refs: exchange_kernel(counts, *refs), out_shape=[j...]
    concatenate x4 -> x0, other arithmetic: 9.64 us -> none  [the longest x2 7.06 us: with_halo(): jnp.concatenate([lax.ppermute(tail, axis, [(i, (i + 1) % count) for i in...]
    div x7 -> x0, other arithmetic: 4.39 us -> none  [the longest x2 1.47 us: local(): (coriolis[0] + circulation_first / triangle_area[0]) / height_first]
    another operation x6 -> x0, other arithmetic: 3.94 us -> none  [the longest x5 2.87 us: local(): jnp.stack([mean_zero - UPWIND_FACTOR * inner_velocity[0] * grad_zero, mea...]
    add x3 -> x0, other arithmetic: 2.89 us -> none  [the longest x1 1.68 us: local(): energy_total = energy_total + weight_now * kinetic]
    ppermute x2 -> x0, local copies, waits for them, and re-layouts: 2.66 us -> none  [the longest x1 1.68 us: with_halo(): lax.ppermute(head, axis, [((i + 1) % count, i) for i in range(count)])]
  transfers between devices with their start and end apart: 26 -> 0, of which waited for: 11 -> 0; matrix products, arithmetic and copies ran while one was open for 14% -> 0% of each run, Pallas kernels for 0% -> 0%
where the time goes in v1:
time: 21 us; the launch traced here: 20.7 us
  Pallas kernels  20 us (95%)
  between operations  0.64 us (3%)
    pallas_call x1, Pallas kernels, exchange(): pl.pallas_call(lambda *refs: exchange_kernel(counts, *refs), out_shape=[j...  12 us
    pallas_call x1, Pallas kernels, local(): pl.pallas_call(step_kernel, grid=(levels,), out_shape=[jax.ShapeDtypeStru...  8 us

profile of v1, /device:TPU:0, one launch (start us, length us, event | category | flops | bytes accessed | tf_op | source)
XLA Modules:
  0.0 20.7 jit_solution(17201357871881169788)
XLA Ops:
  0.6 12.0 %exchange.1 = (f32[160,256]{1,0:T(8,128)}, f32[160,256]{1,0:T(8,128)}, f32[32,256]{1,0:T(8,128)}, f32[32,256]{1,0:T(8,128)}, f32[8,256]{1,0:T(8,128)}, /*index=5*/f32[8,256]{1,0:T(8,128)}, f32[8,256]{1,0:T(8,128)}) custom-call(f32[3,8,32,256]{3,2,1,0:T(8,128)} %vel.1, f32[8,32,256]{2,1,0:T(8,128)} %th.1, f32[3,8,32,256]{3,2,1,0:T(8,128)} %vt.1, ...), custom_call_target="tpu_custom_call" | custom-call | tf_op jit(solution)/shard_map/exchange/pallas_call | solution.py:148
  12.7 8.0 %step.1 = (f32[2,8,32,256]{3,2,1,0:T(8,128)}, f32[8,32,256]{2,1,0:T(8,128)}, f32[8,32,256]{2,1,0:T(8,128)}, f32[3,8,32,256]{3,2,1,0:T(8,128)}) custom-call(f32[3,8,32,256]{3,2,1,0:T(8,128)} %vel.1, f32[8,32,256]{2,1,0:T(8,128)} %th.1, f32[3,8,32,256]{3,2,1,0:T(8,128)} %vt.1, f32[8,32,256]{2,1,0:T(8,128)} %tt.1, f32[3,32,256]{2,1,0:T(8,128)} %cd.1, ...), custom_call_target="tpu_custom_call" | custom-call | tf_op jit(solution)/shard_map/step/pallas_call | solution.py:367

commit v2 on v1

--- a/solution.py
+++ b/solution.py
@@ -9,6 +9,7 @@
 LANE = 128
 COMPS = 8
 GEO = 14
+DEPTH = 2
 LANE_STEP = 2 * COMPS
 MESH = pl.DeviceIdType.MESH
 
@@ -96,21 +97,6 @@
             p_right[rs, cs] = ra
             p_left[rs, cs] = la
 
-    for i in (4, 5, 6, 7):
-        loads[i].wait()
-    pack_rows(geo, levels * LANE_STEP)
-    pack_cols([(2 * k, f) for k, f in enumerate(geo)], 1)
-    for i in (0, 1, 2, 3):
-        loads[i].wait()
-    items = []
-    for l in range(levels):
-        comps = level_comps(l)
-        items += [(l * LANE_STEP + 2 * k, f) for k, f in enumerate(comps)]
-    pack_cols(items, 0)
-    for l in range(levels):
-        pack_rows(level_comps(l), l * LANE_STEP)
-
-    pl.semaphore_wait(barrier, len(near))
     plan = [
         (p_bot, o_bot, (up, px)),
         (p_top, o_top, (down, px)),
@@ -131,7 +117,23 @@
         )
         for i, (src, dst, (y, x)) in enumerate(plan)
     ]
-    for copy in copies:
+    for i in (4, 5, 6, 7):
+        loads[i].wait()
+    pack_rows(geo, levels * LANE_STEP)
+    pack_cols([(2 * k, f) for k, f in enumerate(geo)], 1)
+    for i in (0, 1, 2, 3):
+        loads[i].wait()
+    for l in range(levels):
+        pack_rows(level_comps(l), l * LANE_STEP)
+    pl.semaphore_wait(barrier, len(near))
+    for copy in copies[:2]:
+        copy.start()
+    items = []
+    for l in range(levels):
+        comps = level_comps(l)
+        items += [(l * LANE_STEP + 2 * k, f) for k, f in enumerate(comps)]
+    pack_cols(items, 0)
+    for copy in copies[2:]:
         copy.start()
     for copy in copies:
         copy.wait()
@@ -206,8 +208,6 @@
         q, g = k % 4, k // 4
 
         def make(r, c):
-            if r < nr and c < nc:
-                return own(*at(r, c))
             if c < nc:
                 b, t = band_bot[at(g, c)], band_top[at(g, c)]
                 m = jnp.where((sub == 2 * q) | (sub == 2 * q + 1), b, t)
@@ -216,7 +216,13 @@
             m = jnp.where((lane == 2 * k) | (lane == 2 * k + 1), rt, lt)
             return pltpu.roll(m, (-2 * k) % LANE, 1) if k else m
 
-        return Field(grid, make)
+        halo = Field(grid, make)
+
+        def tile(r, c):
+            r, c = r % grid[0], c % grid[1]
+            return own(*at(r, c)) if r < nr and c < nc else halo(r, c)
+
+        return tile
 
     def side_of(tile, turn):
         cs = slice(tile * LANE, (tile + 1) * LANE)
@@ -262,96 +268,98 @@
                         scale[(k,) + at(r, c)] = (-0.5 / 36.0) / f[k](r, c)
                     scale[(3,) + at(r, c)] = 1.0 / area[at(r, c)]
 
-    turn_by = lax.rem(LANE - level * LANE_STEP, LANE)
+    turn_by = lax.rem(LANE - level * (DEPTH * LANE_STEP), LANE)
     side = side_of(0, lambda x: pltpu.roll(x, turn_by, 1))
-    owns = (
-        [view(vel, k, 0) for k in range(3)]
-        + [view(th, 0)]
-        + [view(vt, k, 0) for k in range(3)]
-        + [view(tt, 0)]
-    )
-    x = [extended(own, k, bot, top, side) for k, own in enumerate(owns)]
-    v, h, t, g = x[0:3], x[3], x[4:7], x[7]
-
-    def geo_tile(k):
-        return lambda r, c: geo[(k,) + at(r % grid[0], c % grid[1])]
-
-    dist = [geo_tile(k) for k in range(3)]
-    ew = [geo_tile(3 + k) for k in range(3)]
-    kt = [geo_tile(6 + k) for k in range(6)]
-    ct = [geo_tile(12 + k) for k in range(2)]
-
-    def parts(vv, hh):
-        flux = [lift(lambda a, b: a * b, vv[k], dist[k]) for k in range(3)]
-        c0 = lift(lambda a, b, c: a + b - c, flux[0], row_shift(flux[2], 1), flux[1])
-        c1 = lift(
-            lambda a, b, c: a - b - c, flux[1], flux[2], col_shift(row_shift(flux[0], -1), 1)
+    for u in range(DEPTH):
+        owns = (
+            [view(vel, k, u) for k in range(3)]
+            + [view(th, u)]
+            + [view(vt, k, u) for k in range(3)]
+            + [view(tt, u)]
         )
-        hc = col_shift(hh, 1)
-        hr = row_shift(hh, 1)
-        hd = row_shift(hc, -1)
-        mix = lambda a, b, c, p, q, s: a * p + b * q + c * s
-        h0 = lift(mix, kt[0], kt[1], kt[2], hh, hr, hc)
-        h1 = lift(mix, kt[3], kt[4], kt[5], hh, hc, hd)
-        return (c0, c1), (h0, h1)
-
-    cv, hv = parts(v, h)
-    cw, hw = parts(t, g)
-
-    def potential(k):
-        def make(r, c):
-            a0 = ct[k](r, c) + cv[k](r, c)
-            a1 = cw[k](r, c)
-            b0 = hv[k](r, c)
-            b1 = hw[k](r, c)
-            first = a0 / b0
-            mid = (a0 + 0.5 * a1) / (b0 + 0.5 * b1)
-            end = (a0 + a1) / (b0 + b1)
-            late = 2.0 * mid + end
-            return first + 2.0 * mid + late, late
-
-        both = Field(grid, make)
-        return Field(grid, lambda r, c: both(r, c)[0]), Field(grid, lambda r, c: both(r, c)[1])
-
-    p0, q0 = potential(0)
-    p1, q1 = potential(1)
-    add = lambda a, b: a + b
-    add3 = lambda a, b, c: a + b + c
-
-    def cell(f0, f1):
-        f0_up = row_shift(f0, -1)
-        f1_down = row_shift(f1, 1)
-        pair = lift(add, f0, f1)
-        return lift(add3, pair, f0_up, col_shift(lift(add, pair, f1_down), -1)), f0_up, f1_down, pair
-
-    cc, p0_up, p1_down, pair = cell(p0, p1)
-    dd = cell(q0, q1)[0]
-    p1_low = col_shift(p1_down, -1)
-
-    def neighbours(f):
-        fc = col_shift(f, 1)
-        return row_shift(f, 1), fc, row_shift(fc, -1)
-
-    cn, dn = neighbours(cc), neighbours(dd)
-    ends = [lift(add, p0, p1_low), pair, lift(add, p1, p0_up)]
-    en = [
-        lift(lambda w, a, b: w * (a * (a + b) + (1.0 / 3.0) * (b * b)), ew[k], v[k], t[k])
-        for k in range(3)
-    ]
-    e_up = row_shift(en[0], -1)
-    e_low = col_shift(lift(add, en[1], row_shift(en[2], 1)), -1)
-
-    for r in range(nr):
-        for c in range(nc):
-            p = at(r, c)
-            o_vert[(0, 0) + p] = p0(r, c) * (1.0 / 6.0)
-            o_vert[(1, 0) + p] = p1(r, c) * (1.0 / 6.0)
-            total = en[0](r, c) + en[1](r, c) + en[2](r, c) + e_up(r, c) + e_low(r, c)
-            o_kin[(0,) + p] = total * scale[(3,) + p]
-            o_cell[(0,) + p] = cc(r, c) * (1.0 / 36.0)
-            for k in range(3):
-                slope = v[k](r, c) * (cn[k](r, c) - cc(r, c)) + t[k](r, c) * (dn[k](r, c) - dd(r, c))
-                o_edge[(k, 0) + p] = ends[k](r, c) * (1.0 / 12.0) + scale[(k,) + p] * slope
+        x = [extended(own, u * COMPS + k, bot, top, side) for k, own in enumerate(owns)]
+        v, h, t, g = x[0:3], x[3], x[4:7], x[7]
+
+        def geo_tile(k):
+            return lambda r, c: geo[(k,) + at(r % grid[0], c % grid[1])]
+
+        dist = [geo_tile(k) for k in range(3)]
+        ew = [geo_tile(3 + k) for k in range(3)]
+        kt = [geo_tile(6 + k) for k in range(6)]
+        ct = [geo_tile(12 + k) for k in range(2)]
+
+        def parts(vv, hh):
+            flux = [lift(lambda a, b: a * b, vv[k], dist[k]) for k in range(3)]
+            c0 = lift(lambda a, b, c: a + b - c, flux[0], row_shift(flux[2], 1), flux[1])
+            c1 = lift(
+                lambda a, b, c: a - b - c, flux[1], flux[2], col_shift(row_shift(flux[0], -1), 1)
+            )
+            hc = col_shift(hh, 1)
+            hr = row_shift(hh, 1)
+            hd = row_shift(hc, -1)
+            mix = lambda a, b, c, p, q, s: a * p + b * q + c * s
+            h0 = lift(mix, kt[0], kt[1], kt[2], hh, hr, hc)
+            h1 = lift(mix, kt[3], kt[4], kt[5], hh, hc, hd)
+            return (c0, c1), (h0, h1)
+
+        cv, hv = parts(v, h)
+        cw, hw = parts(t, g)
+
+        def potential(k):
+            def make(r, c):
+                a0 = ct[k](r, c) + cv[k](r, c)
+                a1 = cw[k](r, c)
+                b0 = hv[k](r, c)
+                b1 = hw[k](r, c)
+                bm, be = b0 + 0.5 * b1, b0 + b1
+                m = bm * be
+                scale_all = 1.0 / (b0 * m)
+                mid = (a0 + a0 + a1) * (b0 * be)
+                late = mid + (a0 + a1) * (b0 * bm)
+                return (a0 * m + mid + late) * scale_all, late * scale_all
+
+            both = Field(grid, make)
+            return Field(grid, lambda r, c: both(r, c)[0]), Field(grid, lambda r, c: both(r, c)[1])
+
+        p0, q0 = potential(0)
+        p1, q1 = potential(1)
+        add = lambda a, b: a + b
+        add3 = lambda a, b, c: a + b + c
+
+        def cell(f0, f1):
+            f0_up = row_shift(f0, -1)
+            f1_down = row_shift(f1, 1)
+            pair = lift(add, f0, f1)
+            return lift(add3, pair, f0_up, col_shift(lift(add, pair, f1_down), -1)), f0_up, f1_down, pair
+
+        cc, p0_up, p1_down, pair = cell(p0, p1)
+        dd = cell(q0, q1)[0]
+        p1_low = col_shift(p1_down, -1)
+
+        def neighbours(f):
+            fc = col_shift(f, 1)
+            return row_shift(f, 1), fc, row_shift(fc, -1)
+
+        cn, dn = neighbours(cc), neighbours(dd)
+        ends = [lift(add, p0, p1_low), pair, lift(add, p1, p0_up)]
+        en = [
+            lift(lambda w, a, b: w * (a * (a + b) + (1.0 / 3.0) * (b * b)), ew[k], v[k], t[k])
+            for k in range(3)
+        ]
+        e_up = row_shift(en[0], -1)
+        e_low = col_shift(lift(add, en[1], row_shift(en[2], 1)), -1)
+
+        for r in range(nr):
+            for c in range(nc):
+                p = at(r, c)
+                o_vert[(0, u) + p] = p0(r, c) * (1.0 / 6.0)
+                o_vert[(1, u) + p] = p1(r, c) * (1.0 / 6.0)
+                total = en[0](r, c) + en[1](r, c) + en[2](r, c) + e_up(r, c) + e_low(r, c)
+                o_kin[(u,) + p] = total * scale[(3,) + p]
+                o_cell[(u,) + p] = cc(r, c) * (1.0 / 36.0)
+                for k in range(3):
+                    slope = v[k](r, c) * (cn[k](r, c) - cc(r, c)) + t[k](r, c) * (dn[k](r, c) - dd(r, c))
+                    o_edge[(k, u) + p] = ends[k](r, c) * (1.0 / 12.0) + scale[(k,) + p] * slope
 
 
 def local(counts, vel, th, vt, tt, cd, el, area, kite, cor):
@@ -359,14 +367,14 @@
     levels, rows, cols = th.shape
     f32 = jnp.float32
     whole = lambda a: pl.BlockSpec(a.shape, lambda l: (0,) * a.ndim)
-    three = pl.BlockSpec((3, 1, rows, cols), lambda l: (0, l, 0, 0))
-    two = pl.BlockSpec((2, 1, rows, cols), lambda l: (0, l, 0, 0))
-    one = pl.BlockSpec((1, rows, cols), lambda l: (l, 0, 0))
-    band = pl.BlockSpec((LANE_STEP, cols), lambda l: (l, 0))
+    three = pl.BlockSpec((3, DEPTH, rows, cols), lambda l: (0, l, 0, 0))
+    two = pl.BlockSpec((2, DEPTH, rows, cols), lambda l: (0, l, 0, 0))
+    one = pl.BlockSpec((DEPTH, rows, cols), lambda l: (l, 0, 0))
+    band = pl.BlockSpec((DEPTH * LANE_STEP, cols), lambda l: (l, 0))
     gband = pl.BlockSpec((32, cols), lambda l: (levels * LANE_STEP // 32, 0))
     return pl.pallas_call(
         step_kernel,
-        grid=(levels,),
+        grid=(levels // DEPTH,),
         out_shape=[
             jax.ShapeDtypeStruct((2, levels, rows, cols), f32),
             jax.ShapeDtypeStruct((levels, rows, cols), f32),

time: 21 us -> 20 us (0.952)
  Pallas kernels: 20 us -> 19.2 us
    pallas_call x1, Pallas kernels: 8 us -> 7.33 us  [local(): pl.pallas_call(step_kernel, grid=(levels // DEPTH,), out_shape=[jax.Shape...]
where the time goes in v2:
time: 20 us; the launch traced here: 19.8 us
  Pallas kernels  19.2 us (96%)
  between operations  0.64 us (3%)
    pallas_call x1, Pallas kernels, exchange(): pl.pallas_call(lambda *refs: exchange_kernel(counts, *refs), out_shape=[j...  11.9 us
    pallas_call x1, Pallas kernels, local(): pl.pallas_call(step_kernel, grid=(levels // DEPTH,), out_shape=[jax.Shape...  7.33 us

profile of v2, /device:TPU:0, one launch (start us, length us, event | category | flops | bytes accessed | tf_op | source)
XLA Modules:
  0.0 19.8 jit_solution(14418759220974245245)
XLA Ops:
  0.6 11.9 %exchange.1 = (f32[160,256]{1,0:T(8,128)}, f32[160,256]{1,0:T(8,128)}, f32[32,256]{1,0:T(8,128)}, f32[32,256]{1,0:T(8,128)}, f32[8,256]{1,0:T(8,128)}, /*index=5*/f32[8,256]{1,0:T(8,128)}, f32[8,256]{1,0:T(8,128)}) custom-call(f32[3,8,32,256]{3,2,1,0:T(8,128)} %vel.1, f32[8,32,256]{2,1,0:T(8,128)} %th.1, f32[3,8,32,256]{3,2,1,0:T(8,128)} %vt.1, ...), custom_call_target="tpu_custom_call" | custom-call | tf_op jit(solution)/shard_map/exchange/pallas_call | solution.py:150
  12.5 7.3 %step.1 = (f32[2,8,32,256]{3,2,1,0:T(8,128)}, f32[8,32,256]{2,1,0:T(8,128)}, f32[8,32,256]{2,1,0:T(8,128)}, f32[3,8,32,256]{3,2,1,0:T(8,128)}) custom-call(f32[3,8,32,256]{3,2,1,0:T(8,128)} %vel.1, f32[8,32,256]{2,1,0:T(8,128)} %th.1, f32[3,8,32,256]{3,2,1,0:T(8,128)} %vt.1, f32[8,32,256]{2,1,0:T(8,128)} %tt.1, f32[3,32,256]{2,1,0:T(8,128)} %cd.1, ...), custom_call_target="tpu_custom_call" | custom-call | tf_op jit(solution)/shard_map/step/pallas_call | solution.py:375
